TPU v7x, 32 devices: a whole 2x2x4 slice. The times are simulated.
32 devices in a mesh: vocab: 8 (over z, y), batch: 4 (over x, core).
Axes of the slice: x: 2, y: 2, z: 4, core: 2. Of those that a mesh axis runs over, the one named last changes fastest.
Arguments:
- latent_vectors: bfloat16 [2048, 4608], P(('batch', 'vocab')), parts along dimension 0, may hold values from -8 to 8
- unembedding_matrix: bfloat16 [18432, 8192], P('batch', 'vocab'), parts along dimension 0, may hold values from -1 to 1
- sampler_heat: float32 [2048], P('batch'), parts along dimension 0, may hold values from 0.1 to 1
Outputs:
- probs: bfloat16 [2048, 8192], P(('batch', 'vocab')), parts along dimension 0
- lse: float32 [2048], P(('batch', 'vocab')), parts along dimension 0
- z_loss: float32 [2048], P(('batch', 'vocab')), parts along dimension 0
There are 4 independent parts, one for each index of `batch`. A program takes and returns all parts, laid end to end along the dimension named above; each array names one. Nothing has to cross between parts.
All inputs are finite; a program needn't handle non-finite values.
Results may differ from a plain program's by a relative error of at most 0.00115.
Values may be sent and summed in bfloat16 or wider, within the bound.
A program may use at most 64 MiB of HBM per device.

v0:
```python
import jax
import jax.numpy as jnp
from jax import lax
from jax.sharding import PartitionSpec as P


def local(latent_vectors, unembedding_matrix, sampler_heat):
    seq_own = latent_vectors.shape[0]
    offset = lax.axis_index("vocab") * seq_own
    logits = jnp.dot(
        lax.all_gather(latent_vectors, "vocab", axis=0, tiled=True),
        unembedding_matrix,
        preferred_element_type=jnp.float32,
    )
    bounded_scores = 30.0 * jnp.tanh(logits / 30.0)
    owned = lax.all_to_all(bounded_scores, "vocab", split_axis=0, concat_axis=1, tiled=True)
    temps = lax.dynamic_slice_in_dim(sampler_heat, offset, seq_own, 0)
    heat_scaled_scores = owned / temps[:, None]
    peak = jnp.max(heat_scaled_scores, axis=1)
    total = jnp.sum(jnp.exp(heat_scaled_scores - peak[:, None]), axis=1)
    lse_own = peak + jnp.log(total)
    probs = jnp.exp(heat_scaled_scores - lse_own[:, None]).astype(jnp.bfloat16)
    z_loss = 0.0001 * lse_own * lse_own
    return (probs, lse_own, z_loss)


def solution(mesh):
    in_specs = (P(("batch", "vocab"), None), P("batch", "vocab"), P("batch"))
    out_specs = (P(("batch", "vocab"), None), P(("batch", "vocab")), P(("batch", "vocab")))
    return jax.shard_map(local, mesh=mesh, in_specs=in_specs, out_specs=out_specs, check_vma=False)
```

profile of v0, /device:TPU:0, one launch (start us, length us, event | category | flops | bytes accessed | tf_op | source)
XLA Modules:
  0.0 163.4 jit_solution(3350614082642482357)
XLA Ops:
  7.2 0.0 all-gather.2.cloned.1.call-start
  7.2 0.7 all-gather.2.cloned.1.call-update
  7.9 84.3 %all-gather.2.cloned.1.call-done = bf16[512,4608]{1,0:T(8,128)(2,1)} async-done(((bf16[64,4608]{1,0:T(8,128)(2,1)}), bf16[512,4608]{1,0:T(8,128)(2,1)}) %all-gather.2.cloned.1.call-update) | async-done | bytes 4718608 | tf_op jit(solution)/shard_map/all_gather | solution.py:11
  92.2 10.0 %tanh_multiply_fusion = f32[512,1024]{1,0:T(8,128)} fusion(bf16[512,4608]{1,0:T(8,128)(2,1)} %all-gather.2.cloned.1.call-done, bf16[4608,1024]{1,0:T(8,128)(2,1)} %param.4), kind=kOutput, calls=%fused_computation.3 | convolution fusion | flops 4832886784 | bytes 16252928 | tf_op jit(solution)/shard_map/dot_general | solution.py:10
  102.3 3.6 %all-to-all-start = ((f32[8,64,1024]{2,1,0:T(8,128)}), f32[8,64,1024]{2,1,0:T(8,128)S(1)}, u32[]{:S(2)}, u32[]{:S(2)}) async-start(f32[8,64,1024]{2,1,0:T(8,128)} %bitcast.13), calls=%async_computation | async-start | bytes 4194304 | tf_op jit(solution)/shard_map/all_to_all | solution.py:16
  105.9 0.8 dynamic_slice.3
  106.6 46.9 %all-to-all-done = f32[8,64,1024]{2,1,0:T(8,128)S(1)} async-done(((f32[8,64,1024]{2,1,0:T(8,128)}), f32[8,64,1024]{2,1,0:T(8,128)S(1)}, u32[]{:S(2)}, u32[]{:S(2)}) %all-to-all-start) | async-done | bytes 2097184 | tf_op jit(solution)/shard_map/all_to_all | solution.py:16
  153.5 0.2 copy.7
  153.7 0.4 fusion
  154.1 0.5 exponential_reduce_fusion
  154.6 0.5 multiply_multiply_fusion
  155.2 0.0 copy-start
  155.2 1.4 exponential_convert_fusion
  156.5 0.0 copy-done
Async XLA Ops:
  7.2 85.1 %all-gather.2.cloned.1.call-start = ((), (), s32[]{:S(2)}) async-start(), calls=%async_computation.1 | async-start | bytes 5308416 | tf_op jit(solution)/shard_map/all_gather | solution.py:11
  102.3 51.2 %all-to-all-start = ((f32[8,64,1024]{2,1,0:T(8,128)}), f32[8,64,1024]{2,1,0:T(8,128)S(1)}, u32[]{:S(2)}, u32[]{:S(2)}) async-start(f32[8,64,1024]{2,1,0:T(8,128)} %bitcast.13), calls=%async_computation | async-start | bytes 4194304 | tf_op jit(solution)/shard_map/all_to_all | solution.py:16
  155.2 1.4 copy-start
Sparse Core Ops, SparseCore 0:
  10.2 82.0 all-gather.1
where the time goes:
time: 164 us; the launch traced here: 163 us
  waiting for transfers between devices  132 us (80%)
  between operations  14.1 us (9%)
  matrix products  10 us (6%)
  starting transfers between devices  3.64 us (2%)
  other arithmetic  2.78 us (2%)
    all_gather x1, waiting for transfers between devices, local(): lax.all_gather(latent_vectors, 'vocab', axis=0, tiled=True)  84.3 us
    all_to_all x1, waiting for transfers between devices, local(): lax.all_to_all(bounded_scores, 'vocab', split_axis=0, concat_axis=1, tile...  46.9 us
    dot_general x1, matrix products, local(): jnp.dot(lax.all_gather(latent_vectors, 'vocab', axis=0, tiled=True), unem...  10 us
    all_to_all x1, starting transfers between devices, local(): lax.all_to_all(bounded_scores, 'vocab', split_axis=0, concat_axis=1, tile...  3.6 us
  transfers between devices with their start and end apart: 2, of which 2 were waited for; matrix products, arithmetic and copies ran while one was open for 0% of the time, Pallas kernels for 0%

commit v1 on v0

v1 whole, which is shorter than its diff:
```python
import functools

import jax
import jax.numpy as jnp
from jax import lax
from jax.experimental import pallas as pl
from jax.experimental.pallas import tpu as pltpu
from jax.sharding import PartitionSpec as P

MESH = pl.DeviceIdType.MESH
UP, DOWN, SIDE = 0, 1, 2


def each(count, body):
    if count <= 8:
        for k in range(count):
            body(k)
    else:
        lax.fori_loop(0, count, lambda k, c: (body(k), c)[1], 0)


def kernel(n, waves, x_ref, w_hbm, heat_ref, probs_ref, lse_ref, w_ref, buf, scaled, outbox, stats, lse_col,
           w_sem, own_sem, ag_send, ag_recv, st_send, st_recv, pr_send, pr_recv):
    me = lax.axis_index("vocab")
    line = n // 2
    z, y = me // 2, lax.rem(me, 2)
    seq = x_ref.shape[0]
    rows = seq // waves
    span = n * rows
    cols = w_ref.shape[1]
    tile = min(cols, 256)

    barrier = pltpu.get_barrier_semaphore()

    def greet(k):
        pl.semaphore_signal(barrier, inc=1, device_id={"vocab": lax.rem(me + k + 1, n)}, device_id_type=MESH)

    each(n - 1, greet)
    weights = pltpu.make_async_copy(w_hbm, w_ref, w_sem)
    weights.start()
    for w in range(waves):
        pltpu.make_async_copy(x_ref.at[pl.ds(w * rows, rows)], buf.at[w, me], own_sem.at[w]).start()
    for w in range(waves):
        pltpu.make_async_copy(x_ref.at[pl.ds(w * rows, rows)], buf.at[w, me], own_sem.at[w]).wait()
    pl.semaphore_wait(barrier, n - 1)

    def hop(w, block, way):
        target = {UP: lax.rem(me + 2, n), DOWN: lax.rem(me + n - 2, n), SIDE: me + 1 - 2 * y}[way]
        return pltpu.make_async_remote_copy(
            src_ref=buf.at[w, block], dst_ref=buf.at[w, block], send_sem=ag_send.at[w, block, way],
            recv_sem=ag_recv.at[w, block], device_id={"vocab": target}, device_id_type=MESH)

    def send_own(w):
        @pl.when(z < line - 1)
        def _():
            hop(w, me, UP).start()

        @pl.when(z > 0)
        def _():
            hop(w, me, DOWN).start()

        hop(w, me, SIDE).start()

    def relay(w, k):
        @pl.when(z >= k)
        def _():
            block = (z - k) * 2 + y
            hop(w, block, SIDE).wait_recv()

            @pl.when(z < line - 1)
            def _():
                hop(w, block, UP).start()

            hop(w, block, SIDE).start()

        @pl.when(z + k < line)
        def _():
            block = (z + k) * 2 + y
            hop(w, block, SIDE).wait_recv()

            @pl.when(z > 0)
            def _():
                hop(w, block, DOWN).start()

            hop(w, block, SIDE).start()

    def stat_copy(w, k):
        return pltpu.make_async_remote_copy(
            src_ref=stats.at[w, me], dst_ref=stats.at[w, me], send_sem=st_send.at[w, k],
            recv_sem=st_recv.at[w, me], device_id={"vocab": lax.rem(me + k + 1, n)}, device_id_type=MESH)

    def stat_wait(w, k):
        other = lax.rem(me + k + 1, n)
        pltpu.make_async_remote_copy(
            src_ref=stats.at[w, other], dst_ref=stats.at[w, other], send_sem=st_send.at[w, k],
            recv_sem=st_recv.at[w, other], device_id={"vocab": other}, device_id_type=MESH).wait_recv()

    def out_at(w, owner):
        return probs_ref.at[pl.ds(w * rows, rows), pl.ds(pl.multiple_of(owner * cols, cols), cols)]

    def prob_copy(w, k):
        other = lax.rem(me + k + 1, n)
        return pltpu.make_async_remote_copy(
            src_ref=outbox.at[w, other], dst_ref=out_at(w, me), send_sem=pr_send.at[w, k],
            recv_sem=pr_recv.at[w, me], device_id={"vocab": other}, device_id_type=MESH)

    def prob_wait(w, k):
        other = lax.rem(me + k + 1, n)
        pltpu.make_async_remote_copy(
            src_ref=outbox.at[w, other], dst_ref=out_at(w, other), send_sem=pr_send.at[w, k],
            recv_sem=pr_recv.at[w, other], device_id={"vocab": other}, device_id_type=MESH).wait_recv()

    def score(w):
        def arrive(k):
            hop(w, k * 2 + 1 - y, SIDE).wait_recv()

        each(line, arrive)
        if w == 0:
            weights.wait()
        hidden = buf[w].reshape(span, buf.shape[3])
        cool = 1.0 / jnp.broadcast_to(heat_ref[w], (8, span)).T[:, :1]

        def column(j, peak):
            at = pl.ds(pl.multiple_of(j * tile, tile), tile)
            logits = jnp.dot(hidden, w_ref[:, at], preferred_element_type=jnp.float32)
            s = 30.0 * jnp.tanh(logits * (1.0 / 30.0)) * cool
            scaled[:, at] = s
            return jnp.maximum(peak, jnp.max(s, axis=1, keepdims=True))

        peak = lax.fori_loop(0, cols // tile, column, jnp.full((span, 1), -jnp.inf, jnp.float32))
        total = jnp.sum(jnp.exp(scaled[...] - peak), axis=1, keepdims=True)
        lane = lax.broadcasted_iota(jnp.int32, (span, 128), 1)
        stats[w, me] = jnp.where(lane == 0, peak, total).T[:8]
        each(n - 1, lambda k: stat_copy(w, k).start())

    def finish(w):
        each(n - 1, lambda k: stat_wait(w, k))
        got = stats[w]
        peaks, totals = got[:, 0, :], got[:, 1, :]
        peak = jnp.max(peaks, axis=0, keepdims=True)
        lse = peak + jnp.log(jnp.sum(totals * jnp.exp(peaks - peak), axis=0, keepdims=True))
        lse = jnp.broadcast_to(lse, (8, span)).T[:, :1]
        probs = jnp.exp(scaled[...] - lse).astype(jnp.bfloat16)
        outbox[w] = probs.reshape(n, rows, cols)
        each(n - 1, lambda k: prob_copy(w, k).start())
        lse_col[...] = jnp.broadcast_to(lse, (span, 128)).reshape(n, rows, 128)
        lse_ref[pl.ds(w * rows, rows), :] = lse_col[me]
        probs_ref[pl.ds(w * rows, rows), pl.ds(pl.multiple_of(me * cols, cols), cols)] = outbox[w, me]

    send_own(0)
    for w in range(waves):
        todo = []
        if w >= 1:
            todo = [functools.partial(score, w - 1), functools.partial(finish, w - 1)]
        if line - 1 <= 8:
            for k in range(1, line):
                relay(w, k)
                if k == 1 and w + 1 < waves:
                    send_own(w + 1)
                if todo:
                    todo.pop(0)()
        else:
            if w + 1 < waves:
                send_own(w + 1)
            each(line - 1, lambda k: relay(w, k + 1))
        while todo:
            todo.pop(0)()
    score(waves - 1)
    finish(waves - 1)

    for w in range(waves):
        each(n - 1, lambda k: prob_wait(w, k))

        def drain(k):
            block = k * 2 + y

            @pl.when(jnp.logical_and(z < line - 1, k <= z))
            def _():
                hop(w, block, UP).wait_send()

            @pl.when(jnp.logical_and(z > 0, k >= z))
            def _():
                hop(w, block, DOWN).wait_send()

            hop(w, block, SIDE).wait_send()

        each(line, drain)
        each(n - 1, lambda k: stat_copy(w, k).wait_send())
        each(n - 1, lambda k: prob_copy(w, k).wait_send())


def solution(mesh):
    n = mesh.shape["vocab"]

    def local(latent_vectors, unembedding_matrix, sampler_heat):
        seq, depth = latent_vectors.shape
        cols = unembedding_matrix.shape[1]
        waves = max(1, seq // 32)
        rows = seq // waves
        span = n * rows
        heat = sampler_heat.reshape(n, waves, rows).transpose(1, 0, 2).reshape(waves, 1, span)
        vmem = pl.BlockSpec(memory_space=pltpu.VMEM)
        dma = pltpu.SemaphoreType.DMA
        probs, lse = pl.pallas_call(
            functools.partial(kernel, n, waves),
            out_shape=(jax.ShapeDtypeStruct((seq, n * cols), jnp.bfloat16),
                       jax.ShapeDtypeStruct((seq, 128), jnp.float32)),
            in_specs=[vmem, pl.BlockSpec(memory_space=pl.ANY), vmem],
            out_specs=(vmem, vmem),
            scratch_shapes=[
                pltpu.VMEM((depth, cols), jnp.bfloat16),
                pltpu.VMEM((waves, n, rows, depth), jnp.bfloat16),
                pltpu.VMEM((span, cols), jnp.float32),
                pltpu.VMEM((waves, n, rows, cols), jnp.bfloat16),
                pltpu.VMEM((waves, n, 8, span), jnp.float32),
                pltpu.VMEM((n, rows, 128), jnp.float32),
                dma, dma((waves,)),
                dma((waves, n, 3)), dma((waves, n)),
                dma((waves, n - 1)), dma((waves, n)),
                dma((waves, n - 1)), dma((waves, n)),
            ],
            compiler_params=pltpu.CompilerParams(
                collective_id=0, has_side_effects=True, vmem_limit_bytes=56 * 1024 * 1024),
        )(latent_vectors, unembedding_matrix, heat)
        lse = lse[:, 0]
        return probs, lse, 0.0001 * lse * lse

    in_specs = (P(("batch", "vocab"), None), P("batch", "vocab"), P("batch"))
    out_specs = (P(("batch", "vocab"), None), P(("batch", "vocab")), P(("batch", "vocab")))
    return jax.shard_map(local, mesh=mesh, in_specs=in_specs, out_specs=out_specs, check_vma=False)
```

time: 164 us -> 89.7 us (0.55)
  waiting for transfers between devices: 132 us -> 0 us
  Pallas kernels: 0 us -> 83.7 us
  between operations: 14.1 us -> 0.65 us
  matrix products: 10 us -> 0 us
  starting transfers between devices: 3.64 us -> 0 us
  local copies, waits for them, and re-layouts: 1 us -> 4.56 us
  other arithmetic: 2.78 us -> 0.51 us
    all_gather x1 -> x0, waiting for transfers between devices: 84.3 us -> none  [local(): lax.all_gather(latent_vectors, 'vocab', axis=0, tiled=True)]
    pallas_call x0 -> x1, Pallas kernels: none -> 83.7 us  [local(): pl.pallas_call(functools.partial(kernel, n, waves), out_shape=(jax.ShapeD...]
    all_to_all x1 -> x0, waiting for transfers between devices: 46.9 us -> none  [local(): lax.all_to_all(bounded_scores, 'vocab', split_axis=0, concat_axis=1, tile...]
    dot_general x1 -> x0, matrix products: 10 us -> none  [local(): jnp.dot(lax.all_gather(latent_vectors, 'vocab', axis=0, tiled=True), unem...]
    all_to_all x1 -> x0, starting transfers between devices: 3.6 us -> none  [local(): lax.all_to_all(bounded_scores, 'vocab', split_axis=0, concat_axis=1, tile...]
    unnamed x2 -> x3, local copies, waits for them, and re-layouts: 0.01 us -> 2.27 us
  transfers between devices with their start and end apart: 2 -> 0, of which waited for: 2 -> 0; matrix products, arithmetic and copies ran while one was open for 0% -> 0% of each run, Pallas kernels for 0% -> 0%
where the time goes in v1:
time: 89.7 us; the launch traced here: 89.5 us
  Pallas kernels  83.7 us (93%)
  local copies, waits for them, and re-layouts  4.56 us (5%)
    pallas_call x1, Pallas kernels, local(): pl.pallas_call(functools.partial(kernel, n, waves), out_shape=(jax.ShapeD...  83.7 us
    unnamed x3, local copies, waits for them, and re-layouts  2.27 us

profile of v1, /device:TPU:0, one launch (start us, length us, event | category | flops | bytes accessed | tf_op | source)
XLA Modules:
  0.0 89.5 jit_solution(5145684220108052562)
XLA Ops:
  0.6 0.8 reshape.12
  1.4 0.7 reshape.13.heat_ref
  2.1 83.7 %shard_map.58 = (bf16[64,8192]{1,0:T(8,128)(2,1)}, f32[64,128]{1,0:T(8,128)}) custom-call(bf16[64,4608]{1,0:T(8,128)(2,1)} %x_ref.1, bf16[4608,1024]{1,0:T(8,128)(2,1)} %w_hbm.1, f32[2,1,256]{2,1,0:T(1,128)} %reshape.13.heat_ref), custom_call_target="tpu_custom_call" | custom-call | tf_op jit(solution)/shard_map/pallas_call | solution.py:204
  85.8 0.9 slice_reduce_fusion
  86.7 0.0 copy-start
  86.7 0.5 multiply_multiply_fusion
  87.2 2.3 %copy.8 = bf16[64,8192]{1,0:T(8,128)(2,1)} copy(bf16[64,8192]{1,0:T(8,128)(2,1)} %get-tuple-element.10) | data formatting | bytes 2097152
  89.5 0.0 copy-done
  (1 shorter events, 0.0 us)
Async XLA Ops:
  86.7 2.8 %copy-start = (f32[64]{0:T(128)}, f32[64]{0:T(128)S(1)}, u32[]{:S(2)}) copy-start(f32[64]{0:T(128)S(1)} %slice_reduce_fusion) | copy-start | bytes 772

commit v2 on v1

--- a/solution.py
+++ b/solution.py
@@ -157,7 +157,7 @@
                 relay(w, k)
                 if k == 1 and w + 1 < waves:
                     send_own(w + 1)
-                if todo:
+                if todo and k >= 2:
                     todo.pop(0)()
         else:
             if w + 1 < waves:
@@ -195,7 +195,7 @@
     def local(latent_vectors, unembedding_matrix, sampler_heat):
         seq, depth = latent_vectors.shape
         cols = unembedding_matrix.shape[1]
-        waves = max(1, seq // 32)
+        waves = max(1, seq // 16)
         rows = seq // waves
         span = n * rows
         heat = sampler_heat.reshape(n, waves, rows).transpose(1, 0, 2).reshape(waves, 1, span)

time: 89.7 us -> 94 us (1.048)
  Pallas kernels: 83.7 us -> 88 us
    pallas_call x1, Pallas kernels: 83.7 us -> 88 us  [local(): pl.pallas_call(functools.partial(kernel, n, waves), out_shape=(jax.ShapeD...]
where the time goes in v2:
time: 94 us; the launch traced here: 93.8 us
  Pallas kernels  88 us (94%)
  local copies, waits for them, and re-layouts  4.56 us (5%)
    pallas_call x1, Pallas kernels, local(): pl.pallas_call(functools.partial(kernel, n, waves), out_shape=(jax.ShapeD...  88 us
    unnamed x3, local copies, waits for them, and re-layouts  2.27 us

profile of v2, /device:TPU:0, one launch (start us, length us, event | category | flops | bytes accessed | tf_op | source)
XLA Modules:
  0.0 93.8 jit_solution(6525498524879354339)
XLA Ops:
  0.6 0.8 reshape.12
  1.4 0.7 reshape.13.heat_ref
  2.1 88.0 %shard_map.58 = (bf16[64,8192]{1,0:T(8,128)(2,1)}, f32[64,128]{1,0:T(8,128)}) custom-call(bf16[64,4608]{1,0:T(8,128)(2,1)} %x_ref.1, bf16[4608,1024]{1,0:T(8,128)(2,1)} %w_hbm.1, f32[4,1,128]{2,1,0:T(1,128)} %reshape.13.heat_ref), custom_call_target="tpu_custom_call" | custom-call | tf_op jit(solution)/shard_map/pallas_call | solution.py:204
  90.1 0.9 slice_reduce_fusion
  91.0 0.0 copy-start
  91.0 0.5 multiply_multiply_fusion
  91.5 2.3 %copy.8 = bf16[64,8192]{1,0:T(8,128)(2,1)} copy(bf16[64,8192]{1,0:T(8,128)(2,1)} %get-tuple-element.10) | data formatting | bytes 2097152
  93.8 0.0 copy-done
  (1 shorter events, 0.0 us)
Async XLA Ops:
  91.0 2.8 %copy-start = (f32[64]{0:T(128)}, f32[64]{0:T(128)S(1)}, u32[]{:S(2)}) copy-start(f32[64]{0:T(128)S(1)} %slice_reduce_fusion) | copy-start | bytes 772

commit v3 on v2

--- a/solution.py
+++ b/solution.py
@@ -195,7 +195,7 @@
     def local(latent_vectors, unembedding_matrix, sampler_heat):
         seq, depth = latent_vectors.shape
         cols = unembedding_matrix.shape[1]
-        waves = max(1, seq // 16)
+        waves = max(1, seq // 32)
         rows = seq // waves
         span = n * rows
         heat = sampler_heat.reshape(n, waves, rows).transpose(1, 0, 2).reshape(waves, 1, span)

time: 94 us -> 90.7 us (0.965)
  Pallas kernels: 88 us -> 84.3 us
    pallas_call x1, Pallas kernels: 88 us -> 84.3 us  [local(): pl.pallas_call(functools.partial(kernel, n, waves), out_shape=(jax.ShapeD...]
where the time goes in v3:
time: 90.7 us; the launch traced here: 90 us
  Pallas kernels  84.3 us (93%)
  local copies, waits for them, and re-layouts  4.56 us (5%)
    pallas_call x1, Pallas kernels, local(): pl.pallas_call(functools.partial(kernel, n, waves), out_shape=(jax.ShapeD...  84.3 us
    unnamed x3, local copies, waits for them, and re-layouts  2.27 us

profile of v3, /device:TPU:0, one launch (start us, length us, event | category | flops | bytes accessed | tf_op | source)
XLA Modules:
  0.0 90.0 jit_solution(726879684487063797)
XLA Ops:
  0.6 0.8 reshape.12
  1.4 0.7 reshape.13.heat_ref
  2.1 84.3 %shard_map.58 = (bf16[64,8192]{1,0:T(8,128)(2,1)}, f32[64,128]{1,0:T(8,128)}) custom-call(bf16[64,4608]{1,0:T(8,128)(2,1)} %x_ref.1, bf16[4608,1024]{1,0:T(8,128)(2,1)} %w_hbm.1, f32[2,1,256]{2,1,0:T(1,128)} %reshape.13.heat_ref), custom_call_target="tpu_custom_call" | custom-call | tf_op jit(solution)/shard_map/pallas_call | solution.py:204
  86.4 0.9 slice_reduce_fusion
  87.3 0.0 copy-start
  87.3 0.5 multiply_multiply_fusion
  87.8 2.3 %copy.8 = bf16[64,8192]{1,0:T(8,128)(2,1)} copy(bf16[64,8192]{1,0:T(8,128)(2,1)} %get-tuple-element.10) | data formatting | bytes 2097152
  90.0 0.0 copy-done
  (1 shorter events, 0.0 us)
Async XLA Ops:
  87.3 2.8 %copy-start = (f32[64]{0:T(128)}, f32[64]{0:T(128)S(1)}, u32[]{:S(2)}) copy-start(f32[64]{0:T(128)S(1)} %slice_reduce_fusion) | copy-start | bytes 772

commit v4 on v1

--- a/solution.py
+++ b/solution.py
@@ -153,10 +153,10 @@
         if w >= 1:
             todo = [functools.partial(score, w - 1), functools.partial(finish, w - 1)]
         if line - 1 <= 8:
+            if w + 1 < waves:
+                send_own(w + 1)
             for k in range(1, line):
                 relay(w, k)
-                if k == 1 and w + 1 < waves:
-                    send_own(w + 1)
                 if todo:
                     todo.pop(0)()
         else:

time: 89.7 us -> 90 us (level)
  no operation moved by 1% of the time
where the time goes in v4:
time: 90 us; the launch traced here: 89.7 us
  Pallas kernels  84 us (93%)
  local copies, waits for them, and re-layouts  4.56 us (5%)
    pallas_call x1, Pallas kernels, local(): pl.pallas_call(functools.partial(kernel, n, waves), out_shape=(jax.ShapeD...  84 us
    unnamed x3, local copies, waits for them, and re-layouts  2.27 us

profile of v4, /device:TPU:0, one launch (start us, length us, event | category | flops | bytes accessed | tf_op | source)
XLA Modules:
  0.0 89.7 jit_solution(16845210991732040448)
XLA Ops:
  0.6 0.8 reshape.12
  1.4 0.7 reshape.13.heat_ref
  2.1 84.0 %shard_map.58 = (bf16[64,8192]{1,0:T(8,128)(2,1)}, f32[64,128]{1,0:T(8,128)}) custom-call(bf16[64,4608]{1,0:T(8,128)(2,1)} %x_ref.1, bf16[4608,1024]{1,0:T(8,128)(2,1)} %w_hbm.1, f32[2,1,256]{2,1,0:T(1,128)} %reshape.13.heat_ref), custom_call_target="tpu_custom_call" | custom-call | tf_op jit(solution)/shard_map/pallas_call | solution.py:204
  86.0 0.9 slice_reduce_fusion
  86.9 0.0 copy-start
  86.9 0.5 multiply_multiply_fusion
  87.4 2.3 %copy.8 = bf16[64,8192]{1,0:T(8,128)(2,1)} copy(bf16[64,8192]{1,0:T(8,128)(2,1)} %get-tuple-element.10) | data formatting | bytes 2097152
  89.7 0.0 copy-done
  (1 shorter events, 0.0 us)
Async XLA Ops:
  86.9 2.8 %copy-start = (f32[64]{0:T(128)}, f32[64]{0:T(128)S(1)}, u32[]{:S(2)}) copy-start(f32[64]{0:T(128)S(1)} %slice_reduce_fusion) | copy-start | bytes 772
